TPU v7x, 32 devices: a whole 2x2x4 slice. The times are simulated.
32 devices in a mesh: owner: 4 (over y, core), rows: 8 (over z, x).
Axes of the slice: x: 2, y: 2, z: 4, core: 2. Of those that a mesh axis runs over, the one named last changes fastest.
Arguments:
- train_gate: float32 [64, 2048, 1024], P('owner', 'rows'), may hold values from -0.1875 to 0.1875
- other_gate: bfloat16 [64, 2048, 1024], P('owner', 'rows'), may hold values from -0.0625 to 0.0625
- train_up: float32 [64, 2048, 1024], P('owner', 'rows'), may hold values from -0.1875 to 0.1875
- other_up: bfloat16 [64, 2048, 1024], P('owner', 'rows'), may hold values from -0.0625 to 0.0625
- train_down: float32 [64, 1024, 2048], P('owner', None, 'rows'), may hold values from -0.25 to 0.25
- other_down: bfloat16 [64, 1024, 2048], P('owner', None, 'rows'), may hold values from -0.09375 to 0.09375
- router_weight: float32 [2048, 64], P('rows', 'owner'), may hold values from -0.125 to 0.125
- router_gain: float32 [2048], P('rows'), may hold values from 0.25 to 1.75
Outputs:
- ready_gate: bfloat16 [64, 2048, 1024], P('owner', None, 'rows')
- ready_up: bfloat16 [64, 2048, 1024], P('owner', None, 'rows')
- ready_down: bfloat16 [64, 1024, 2048], P('owner', 'rows')
- scale_gate: float32 [64, 1024], P('owner', 'rows')
- scale_up: float32 [64, 1024], P('owner', 'rows')
- scale_down: float32 [64, 1024], P('owner', 'rows')
- serve_router: bfloat16 [2048, 64], replicated
All inputs are finite; a program needn't handle non-finite values. Where the computation divides by a largest or mean magnitude, that divisor is 1e-20 or more.
Results may differ from a plain program's by a relative error of at most 0.001.
Values may be sent and summed in bfloat16 or wider, within the bound.
A program may use at most 192 MiB of HBM per device.

v0:
```python
import jax
import jax.numpy as jnp
from jax import lax
from jax.sharding import PartitionSpec as P


def shards(
    train_gate, other_gate, train_up, other_up, train_down, other_down, router_weight, router_gain
):
    latest_gate = train_gate + other_gate.astype(jnp.float32)
    latest_up = train_up + other_up.astype(jnp.float32)
    latest_down = train_down + other_down.astype(jnp.float32)
    scale_gate, scale_up, scale_down = lax.pmax(
        (
            jnp.max(jnp.abs(latest_gate), axis=1),
            jnp.max(jnp.abs(latest_up), axis=1),
            jnp.max(jnp.abs(latest_down), axis=2),
        ),
        "rows",
    )
    narrow_gate, narrow_up, narrow_down = (
        (latest_gate / jnp.expand_dims(scale_gate, 1)).astype(jnp.bfloat16),
        (latest_up / jnp.expand_dims(scale_up, 1)).astype(jnp.bfloat16),
        (latest_down / jnp.expand_dims(scale_down, 2)).astype(jnp.bfloat16),
    )
    ready_gate, ready_up = (
        lax.all_to_all(narrow_gate, "rows", split_axis=2, concat_axis=1, tiled=True),
        lax.all_to_all(narrow_up, "rows", split_axis=2, concat_axis=1, tiled=True),
    )
    ready_down = lax.all_to_all(narrow_down, "rows", split_axis=1, concat_axis=2, tiled=True)
    scale_gate = lax.dynamic_slice_in_dim(
        scale_gate, lax.axis_index("rows") * ready_gate.shape[2], ready_gate.shape[2], axis=1
    )
    scale_up = lax.dynamic_slice_in_dim(
        scale_up, lax.axis_index("rows") * ready_up.shape[2], ready_up.shape[2], axis=1
    )
    scale_down = lax.dynamic_slice_in_dim(
        scale_down, lax.axis_index("rows") * ready_down.shape[1], ready_down.shape[1], axis=1
    )
    part_router = (router_weight * router_gain[:, None]).astype(jnp.bfloat16)
    row_router = lax.all_gather(part_router, "rows", axis=0, tiled=True)
    serve_router = lax.all_gather(row_router, "owner", axis=1, tiled=True)
    return (ready_gate, ready_up, ready_down, scale_gate, scale_up, scale_down, serve_router)


def solution(mesh):
    placed = (
        P("owner", "rows", None),
        P("owner", "rows", None),
        P("owner", "rows", None),
        P("owner", "rows", None),
        P("owner", None, "rows"),
        P("owner", None, "rows"),
        P("rows", "owner"),
        P("rows"),
    )
    return jax.shard_map(
        shards,
        mesh=mesh,
        in_specs=placed,
        out_specs=(
            P("owner", None, "rows"),
            P("owner", None, "rows"),
            P("owner", "rows", None),
            P("owner", "rows"),
            P("owner", "rows"),
            P("owner", "rows"),
            P(),
        ),
        check_vma=False,
    )
```

profile of v0, /device:TPU:10, one launch (start us, length us, event | category | flops | bytes accessed | tf_op | source)
XLA Modules:
  0.0 872.9 jit_solution(6322543164802641597)
XLA Ops:
  7.2 0.0 all-reduce.3.cloned.1.call-start
  7.2 17.6 %copy.34 = f32[16,256,1024]{1,0,2:T(8,128)} copy(f32[16,256,1024]{2,1,0:T(8,128)} %param.10) | data formatting | bytes 33554432 | tf_op args[2]
  24.8 12.5 %copy.33 = bf16[16,256,1024]{1,0,2:T(8,128)(2,1)} copy(bf16[16,256,1024]{2,1,0:T(8,128)(2,1)} %param.11) | data formatting | bytes 16777216 | tf_op args[3]
  37.3 17.6 %copy.31 = f32[16,256,1024]{1,0,2:T(8,128)} copy(f32[16,256,1024]{2,1,0:T(8,128)} %param.8) | data formatting | bytes 33554432 | tf_op args[0]
  54.9 12.5 %copy.30 = bf16[16,256,1024]{1,0,2:T(8,128)(2,1)} copy(bf16[16,256,1024]{2,1,0:T(8,128)(2,1)} %param.9) | data formatting | bytes 16777216 | tf_op args[1]
  67.4 0.0 copy-start
  67.4 0.0 copy-start.1
  67.4 0.0 slice-start
  67.4 11.1 %abs_reduce_fusion.1 = f32[16,1024]{0,1:T(8,128)} fusion(f32[16,256,1024]{1,0,2:T(8,128)} %copy.34, bf16[16,256,1024]{1,0,2:T(8,128)(2,1)} %copy.33), kind=kLoop, calls=%fused_computation.4 | loop fusion | flops 16760832 | bytes 25231360 | tf_op jit(solution)/shard_map/reduce_max | solution.py:16
  78.5 2.1 copy-done
  80.6 2.4 copy-done.1
  83.0 0.0 slice-start.1
  83.0 4.3 abs_reduce_fusion.2
  87.3 0.0 slice-done
  87.3 0.0 slice-done.1
  87.3 29.3 %abs_reduce_fusion = f32[16,1024]{0,1:T(8,128)} fusion(f32[16,1024,256]{2,1,0:T(8,128)} %param.12, bf16[16,1024,256]{2,1,0:T(8,128)(2,1)S(1)} %bitcast.14), kind=kLoop, calls=%fused_computation.2 | loop fusion | flops 16760832 | bytes 25231360 | tf_op jit(solution)/shard_map/reduce_max | solution.py:17
  116.5 0.0 all-reduce.3.cloned.1.call-update
  116.6 90.7 %all-reduce.3.cloned.1.call-done = (f32[16,1024]{0,1:T(8,128)}, f32[16,1024]{0,1:T(8,128)}, f32[16,1024]{0,1:T(8,128)}) async-done(((f32[16,1024]{0,1:T(8,128)}, f32[16,1024]{0,1:T(8,128)}, f32[16,1024]{0,1:T(8,128)}), (f32[16,1024]{0,1:T(8,128)}, f32[16,1024]{0,1:T(8,128)}, f32[16,1024]{0,1:T(8,128)})) %all-reduce.3.cloned.1.call-update) | async-done | bytes 196624 | tf_op jit(solution)/shard_map/pmax | solution.py:13
  207.2 20.5 %divide_convert_fusion.1 = (bf16[16,256,1024]{1,0,2:T(8,128)(2,1)}, bf16[16,256,1024]{1,0,2:T(8,128)(2,1)S(1)}) fusion(f32[16,256,1024]{1,0,2:T(8,128)} %copy.34, bf16[16,256,1024]{1,0,2:T(8,128)(2,1)} %copy.33, f32[16,1024]{0,1:T(8,128)} %get-tuple-element.15, f32[16,1024]{0,1:T(8,128)} %get-tuple-element.14, f32[16,256,1024]{1,0,2:T(8,128)} %copy.31, ...), kind=kLoop, calls=%fused_computation.3 | loop fusion | flops 33554432 | bytes 67239936 | tf_op jit(solution)/shard_map/convert_element_type | solution.py:23
  227.8 0.0 copy-start.2
  227.8 185.6 %all_to_all.54 = bf16[16,256,1024]{1,0,2:T(8,128)(2,1)} all-to-all(bf16[16,256,1024]{1,0,2:T(8,128)(2,1)S(1)} %get-tuple-element.18), channel_id=1, replica_groups=mesh['owner'=4,'rows'=8] {'rows'}, dimensions={2} | all-to-all | bytes 16777216 | tf_op jit(solution)/shard_map/all_to_all | solution.py:27
  413.4 7.0 all-to-all-start.1
  420.4 0.0 copy-done.2
  420.4 23.8 %divide_convert_fusion = bf16[16,1024,256]{2,0,1:T(8,128)(2,1)} fusion(f32[16,1024,256]{2,1,0:T(8,128)} %param.12, f32[16,1024]{0,1:T(8,128)S(1)} %copy-done.2, bf16[16,1024,256]{2,1,0:T(8,128)(2,1)} %param.13), kind=kLoop, calls=%fused_computation.1 | loop fusion | flops 16777216 | bytes 33619968 | tf_op jit(solution)/shard_map/convert_element_type | solution.py:24
  444.1 0.0 copy-start.3
  444.1 0.0 copy-start.4
  444.1 155.0 %all-to-all-done.1 = bf16[16,256,1024]{1,0,2:T(8,128)(2,1)} async-done(((bf16[16,256,1024]{1,0,2:T(8,128)(2,1)}), bf16[16,256,1024]{1,0,2:T(8,128)(2,1)}, u32[]{:S(2)}, u32[]{:S(2)}) %all-to-all-start.1) | async-done | bytes 8388640 | tf_op jit(solution)/shard_map/all_to_all | solution.py:28
  599.2 8.3 all-to-all-start.2
  607.5 0.0 copy-done.3
  607.5 0.0 copy-done.4
  607.5 198.8 %all_gather.6 = bf16[2048,16]{0,1:T(8,128)(2,1)S(1)} all-gather(bf16[256,16]{0,1:T(8,128)(2,1)S(1)} %multiply_convert_fusion), channel_id=1, replica_groups=mesh['owner'=4,'rows'=8] {'rows'}, dimensions={0}, use_global_device_ids=true | all-gather | bytes 73728 | tf_op jit(solution)/shard_map/all_gather | solution.py:41
  806.3 6.0 all_gather.7
  812.2 0.8 constant_dynamic-slice_fusion
  813.1 0.7 copy.40
  813.8 0.7 copy.41
  814.4 0.8 constant_dynamic-slice_fusion.2
  815.3 0.7 copy.39
  815.9 12.3 %copy.32 = bf16[16,8,256,128]{3,2,1,0:T(8,128)(2,1)} copy(bf16[16,8,256,128]{2,0,3,1:T(8,128)(2,1)} %bitcast.15) | data formatting | bytes 16777216 | tf_op jit(solution)/shard_map/all_to_all | solution.py:27
  828.2 12.3 %copy.35 = bf16[16,8,256,128]{3,2,1,0:T(8,128)(2,1)} copy(bf16[16,8,256,128]{2,0,3,1:T(8,128)(2,1)} %bitcast.4) | data formatting | bytes 16777216 | tf_op jit(solution)/shard_map/all_to_all | solution.py:28
  840.5 0.0 all-to-all-done.2
  840.5 11.4 %copy.38 = bf16[16,128,8,256]{3,2,1,0:T(8,128)(2,1)} copy(bf16[16,128,8,256]{3,0,1,2:T(8,128)(2,1)} %bitcast.7) | data formatting | bytes 16777216 | tf_op jit(solution)/shard_map/all_to_all | solution.py:30
  851.9 13.4 %all_to_all.50 = bf16[16,128,2048]{2,1,0:T(8,128)(2,1)} reshape(bf16[16,128,8,256]{3,2,1,0:T(8,128)(2,1)} %copy.38) | data formatting | bytes 16777216 | tf_op jit(solution)/shard_map/all_to_all | solution.py:30
  865.3 0.7 copy.53
  (2 shorter events, 0.0 us)
Async XLA Ops:
  7.2 200.1 %all-reduce.3.cloned.1.call-start = ((), (), s32[]{:S(2)}) async-start(), calls=%async_computation.3 | async-start | bytes 3145728 | tf_op jit(solution)/shard_map/pmax | solution.py:13
  67.4 13.2 %copy-start = (f32[16,256,1024]{1,0,2:T(8,128)S(1)}, f32[16,256,1024]{1,0,2:T(8,128)}, u32[]{:S(2)}) copy-start(f32[16,256,1024]{1,0,2:T(8,128)} %copy.31) | copy-start | bytes 50331652
  67.4 15.6 %copy-start.1 = (bf16[16,256,1024]{1,0,2:T(8,128)(2,1)S(1)}, bf16[16,256,1024]{1,0,2:T(8,128)(2,1)}, u32[]{:S(2)}) copy-start(bf16[16,256,1024]{1,0,2:T(8,128)(2,1)} %copy.30) | copy-start | bytes 25165828
  67.4 19.9 %slice-start = ((s8[8388608]{0:T(1024)(128)(4,1)}), s8[4194304]{0:T(1024)(128)(4,1)S(1)}, s32[]{:S(2)}) async-start(s8[8388608]{0:T(1024)(128)(4,1)} %bitcast.13), calls=%async_computation.4 | async-start | bytes 8388608
  83.0 4.3 slice-start.1
  227.8 192.6 %copy-start.2 = (f32[16,1024]{0,1:T(8,128)S(1)}, f32[16,1024]{0,1:T(8,128)}, u32[]{:S(2)}) copy-start(f32[16,1024]{0,1:T(8,128)} %get-tuple-element.16) | copy-start | bytes 196612
  413.4 185.8 %all-to-all-start.1 = ((bf16[16,256,1024]{1,0,2:T(8,128)(2,1)}), bf16[16,256,1024]{1,0,2:T(8,128)(2,1)}, u32[]{:S(2)}, u32[]{:S(2)}) async-start(bf16[16,256,1024]{1,0,2:T(8,128)(2,1)} %get-tuple-element.17), calls=%async_computation.1 | async-start | bytes 16777216 | tf_op jit(solution)/shard_map/all_to_all | solution.py:28
  444.1 163.3 %copy-start.3 = (f32[256,16]{0,1:T(8,128)S(1)}, f32[256,16]{0,1:T(8,128)}, u32[]{:S(2)}) copy-start(f32[256,16]{0,1:T(8,128)} %param.14) | copy-start | bytes 49156
  444.1 163.3 %copy-start.4 = (f32[256]{0:T(256)S(1)}, f32[256]{0:T(256)}, u32[]{:S(2)}) copy-start(f32[256]{0:T(256)} %param.15) | copy-start | bytes 3076
  599.2 241.4 %all-to-all-start.2 = ((bf16[16,1024,256]{2,0,1:T(8,128)(2,1)}), bf16[16,1024,256]{2,0,1:T(8,128)(2,1)}, u32[]{:S(2)}, u32[]{:S(2)}) async-start(bf16[16,1024,256]{2,0,1:T(8,128)(2,1)} %divide_convert_fusion), calls=%async_computation.2 | async-start | bytes 16777216 | tf_op jit(solution)/shard_map/all_to_all | solution.py:30
Sparse Core Ops, SparseCore 0:
  116.7 90.4 all-reduce.2
where the time goes:
time: 880 us; the launch traced here: 873 us
  blocking collectives  390 us (44%)
  waiting for transfers between devices  246 us (28%)
  local copies, waits for them, and re-layouts  118 us (13%)
  other arithmetic  88.9 us (10%)
  starting transfers between devices  15.3 us (2%)
  between operations  14.1 us (2%)
    all_gather x1, blocking collectives, shards(): row_router = lax.all_gather(part_router, 'rows', axis=0, tiled=True)  199 us
    all_to_all x1, blocking collectives, shards(): lax.all_to_all(narrow_gate, 'rows', split_axis=2, concat_axis=1, tiled=True)  186 us
    all_to_all x1, waiting for transfers between devices, shards(): lax.all_to_all(narrow_up, 'rows', split_axis=2, concat_axis=1, tiled=True)  155 us
    pmax x1, waiting for transfers between devices, shards(): lax.pmax((jnp.max(jnp.abs(latest_gate), axis=1), jnp.max(jnp.abs(latest_u...  90.7 us
    unnamed x22, local copies, waits for them, and re-layouts  67.4 us
    reduce_max x1, other arithmetic, shards(): jnp.max(jnp.abs(latest_down), axis=2)  29.3 us
    all_to_all x2, local copies, waits for them, and re-layouts, shards(): lax.all_to_all(narrow_down, 'rows', split_axis=1, concat_axis=2, tiled=True)  24.8 us
    convert_element_type x1, other arithmetic, shards(): (latest_down / jnp.expand_dims(scale_down, 2)).astype(jnp.bfloat16)  23.8 us
  transfers between devices with their start and end apart: 3, of which 2 were waited for; matrix products, arithmetic and copies ran while one was open for 6% of the time, Pallas kernels for 0%

commit v1 on v0

v1 whole, which is shorter than its diff:
```python
import functools

import jax
import jax.numpy as jnp
from jax import lax
from jax.experimental import pallas as pl
from jax.experimental.pallas import tpu as pltpu
from jax.sharding import PartitionSpec as P

LANES = 128
MESH = pl.DeviceIdType.MESH


def widest(x):
    most = jnp.abs(x[:, :LANES])
    for at in range(LANES, x.shape[1], LANES):
        most = jnp.maximum(most, jnp.abs(x[:, at : at + LANES]))
    return jnp.max(most.T, axis=0, keepdims=True)


def maxima_kernel(tg, og, tu, ou, td, od, sg, su, sd):
    for train, other, scale in ((tg, og, sg), (tu, ou, su)):
        latest = train[0] + other[0].astype(jnp.float32)
        scale[0] = jnp.max(jnp.abs(latest), axis=0, keepdims=True)
    sd[0] = widest(td[0] + od[0].astype(jnp.float32))


def narrow_kernel(tg, og, tu, ou, td, od, sg, su, sd, ng, nu, nd):
    parts = ng.shape[0]
    for train, other, scale, out in ((tg, og, sg, ng), (tu, ou, su, nu)):
        share = 1.0 / scale[0]
        wide = out.shape[3]
        latest = (train[0] + other[0].astype(jnp.float32)) * share
        latest = latest.astype(jnp.bfloat16)
        for j in range(parts):
            out[j, 0] = latest[:, j * wide : (j + 1) * wide]
    tall = nd.shape[2]
    share = jnp.broadcast_to(1.0 / sd[0], (LANES, sd.shape[2])).T
    for at in range(0, td.shape[2], LANES):
        here = slice(at, at + LANES)
        latest = (td[0, :, here] + od[0, :, here].astype(jnp.float32)) * share
        latest = latest.astype(jnp.bfloat16)
        for j in range(parts):
            nd[j, 0, :, here] = latest[j * tall : (j + 1) * tall]


def exchange_kernel(parts, ng, nu, nd, rg, ru, rd, send_sem, recv_sem, own_sem):
    me = lax.axis_index("rows")
    barrier = pltpu.get_barrier_semaphore()
    for k in range(1, parts):
        pl.semaphore_signal(
            barrier, inc=1, device_id={"rows": lax.rem(me + k, parts)}, device_id_type=MESH
        )
    pl.semaphore_wait(barrier, parts - 1)

    tall, wide = ng.shape[2], nd.shape[3]
    mine = pl.ds(pl.multiple_of(me * tall, tall), tall)
    columns = pl.ds(pl.multiple_of(me * wide, wide), wide)
    places = (
        (ng, rg.at[:, mine, :]),
        (nu, ru.at[:, mine, :]),
        (nd, rd.at[:, :, columns]),
    )
    copies, own = [], []
    for t, (narrow, place) in enumerate(places):
        for k in range(1, parts):
            peer = lax.rem(me + k, parts)
            copy = pltpu.make_async_remote_copy(
                src_ref=narrow.at[peer],
                dst_ref=place,
                send_sem=send_sem.at[t, k - 1],
                recv_sem=recv_sem.at[t, k - 1],
                device_id={"rows": peer},
                device_id_type=MESH,
            )
            copy.start()
            copies.append(copy)
        copy = pltpu.make_async_copy(narrow.at[me], place, own_sem.at[t])
        copy.start()
        own.append(copy)
    for copy in own + copies:
        copy.wait()


def shards(
    parts, train_gate, other_gate, train_up, other_up, train_down, other_down, router_weight, router_gain
):
    weights = (train_gate, other_gate, train_up, other_up, train_down, other_down)
    experts, tall, inner = train_gate.shape
    wide = train_down.shape[2]
    piece = inner // parts
    f32, bf16 = jnp.float32, jnp.bfloat16

    whole = [pl.BlockSpec((1,) + w.shape[1:], lambda e: (e, 0, 0)) for w in weights]
    row = pl.BlockSpec((1, 1, inner), lambda e: (e, 0, 0))
    read = sum(w.size * w.dtype.itemsize for w in weights)
    maxima = pl.pallas_call(
        maxima_kernel,
        grid=(experts,),
        in_specs=whole,
        out_specs=[row] * 3,
        out_shape=[jax.ShapeDtypeStruct((experts, 1, inner), f32)] * 3,
        cost_estimate=pl.CostEstimate(flops=read, bytes_accessed=read, transcendentals=0),
    )(*weights)
    scales = lax.pmax(tuple(maxima), "rows")

    cut = [(parts, experts, tall, piece)] * 2 + [(parts, experts, piece, wide)]
    narrow = pl.pallas_call(
        narrow_kernel,
        grid=(experts,),
        in_specs=whole + [row] * 3,
        out_specs=[pl.BlockSpec((s[0], 1) + s[2:], lambda e: (0, e, 0, 0)) for s in cut],
        out_shape=[jax.ShapeDtypeStruct(s, bf16) for s in cut],
        cost_estimate=pl.CostEstimate(flops=read, bytes_accessed=2 * read, transcendentals=0),
    )(*weights, *scales)

    anywhere = pl.BlockSpec(memory_space=pl.ANY)
    ready_shape = [(experts, parts * tall, piece)] * 2 + [(experts, piece, parts * wide)]
    ready_gate, ready_up, ready_down = pl.pallas_call(
        functools.partial(exchange_kernel, parts),
        in_specs=[anywhere] * 3,
        out_specs=[anywhere] * 3,
        out_shape=[jax.ShapeDtypeStruct(s, bf16) for s in ready_shape],
        scratch_shapes=[
            pltpu.SemaphoreType.DMA((3, parts - 1)),
            pltpu.SemaphoreType.DMA((3, parts - 1)),
            pltpu.SemaphoreType.DMA((3,)),
        ],
        compiler_params=pltpu.CompilerParams(collective_id=0, has_side_effects=True),
    )(*narrow)

    at = lax.axis_index("rows") * piece
    scale_gate, scale_up, scale_down = (
        lax.dynamic_slice_in_dim(s[:, 0, :], at, piece, axis=1) for s in scales
    )
    part_router = (router_weight * router_gain[:, None]).astype(bf16)
    row_router = lax.all_gather(part_router, "rows", axis=0, tiled=True)
    serve_router = lax.all_gather(row_router, "owner", axis=1, tiled=True)
    return (ready_gate, ready_up, ready_down, scale_gate, scale_up, scale_down, serve_router)


def solution(mesh):
    placed = (
        P("owner", "rows", None),
        P("owner", "rows", None),
        P("owner", "rows", None),
        P("owner", "rows", None),
        P("owner", None, "rows"),
        P("owner", None, "rows"),
        P("rows", "owner"),
        P("rows"),
    )
    return jax.shard_map(
        functools.partial(shards, mesh.shape["rows"]),
        mesh=mesh,
        in_specs=placed,
        out_specs=(
            P("owner", None, "rows"),
            P("owner", None, "rows"),
            P("owner", "rows", None),
            P("owner", "rows"),
            P("owner", "rows"),
            P("owner", "rows"),
            P(),
        ),
        check_vma=False,
    )
```

time: 880 us -> 716 us (0.81)
  Pallas kernels: 0 us -> 603 us
  blocking collectives: 390 us -> 33.9 us
  waiting for transfers between devices: 246 us -> 38.1 us
  local copies, waits for them, and re-layouts: 118 us -> 26.9 us
  other arithmetic: 88.9 us -> 0.01 us
  starting transfers between devices: 15.3 us -> 0.04 us
    pallas_call x0 -> x3, Pallas kernels: none -> 603 us  [the longest x1 542 us: shards(): pl.pallas_call(functools.partial(exchange_kernel, parts), in_specs=[anywh...]
    all_to_all x1 -> x0, blocking collectives: 186 us -> none  [shards(): lax.all_to_all(narrow_gate, 'rows', split_axis=2, concat_axis=1, tiled=True)]
    all_gather x1, blocking collectives: 199 us -> 28.1 us  [shards(): row_router = lax.all_gather(part_router, 'rows', axis=0, tiled=True)]
    all_to_all x2 -> x0, waiting for transfers between devices: 155 us -> none  [the longest x1 155 us: shards(): lax.all_to_all(narrow_up, 'rows', split_axis=2, concat_axis=1, tiled=True)]
    pmax x1, waiting for transfers between devices: 90.7 us -> 38.1 us  [shards(): scales = lax.pmax(tuple(maxima), 'rows')]
    all_to_all x4 -> x0, local copies, waits for them, and re-layouts: 49.4 us -> none  [the longest x2 24.8 us: shards(): lax.all_to_all(narrow_down, 'rows', split_axis=1, concat_axis=2, tiled=True)]
    reduce_max x3 -> x0, other arithmetic: 44.6 us -> none  [the longest x1 29.3 us: shards(): jnp.max(jnp.abs(latest_down), axis=2)]
    convert_element_type x3 -> x1, other arithmetic: 44.3 us -> 0.01 us  [shards(): part_router = (router_weight * router_gain[:, None]).astype(bf16)]
  transfers between devices with their start and end apart: 3 -> 1, of which waited for: 2 -> 1; matrix products, arithmetic and copies ran while one was open for 6% -> 0% of each run, Pallas kernels for 0% -> 0%
where the time goes in v1:
time: 716 us
  Pallas kernels  603 us (84%)
  waiting for transfers between devices  38.1 us (5%)
  blocking collectives  33.9 us (5%)
  local copies, waits for them, and re-layouts  26.9 us (4%)
  between operations  14.1 us (2%)
    pallas_call x1, Pallas kernels, shards(): pl.pallas_call(functools.partial(exchange_kernel, parts), in_specs=[anywh...  542 us
    pmax x1, waiting for transfers between devices, shards(): scales = lax.pmax(tuple(maxima), 'rows')  38.1 us
    pallas_call x1, Pallas kernels, shards(): pl.pallas_call(narrow_kernel, grid=(experts,), in_specs=whole + [row] * 3...  35.8 us
    all_gather x1, blocking collectives, shards(): row_router = lax.all_gather(part_router, 'rows', axis=0, tiled=True)  28.1 us
    pallas_call x1, Pallas kernels, shards(): pl.pallas_call(maxima_kernel, grid=(experts,), in_specs=whole, out_specs=...  25.2 us
    unnamed x8, local copies, waits for them, and re-layouts  24.3 us
  transfers between devices with their start and end apart: 1, of which 1 were waited for; matrix products, arithmetic and copies ran while one was open for 0% of the time, Pallas kernels for 0%

profile of v1, /device:TPU:10, one launch (start us, length us, event | category | flops | bytes accessed | tf_op | source)
XLA Modules:
  0.0 715.9 jit_solution(7024078650153557598)
XLA Ops:
  7.2 0.0 copy-start
  7.2 0.0 copy-start.1
  7.2 0.0 all-reduce.3.cloned.1.call-start
  7.2 25.2 %shard_map.135 = (f32[16,1,1024]{2,1,0:T(1,128)}, f32[16,1,1024]{2,1,0:T(1,128)}, f32[16,1,1024]{2,1,0:T(1,128)}) custom-call(f32[16,256,1024]{2,1,0:T(8,128)} %tg.3, bf16[16,256,1024]{2,1,0:T(8,128)(2,1)} %og.3, f32[16,256,1024]{2,1,0:T(8,128)} %tu.3, bf16[16,256,1024]{2,1,0:T(8,128)(2,1)} %ou.3, f32[16,1024,256]{2,1,0:T(8,128)} %td.3, ...), custom_call_target="tpu_custom_call" | custom-call | flops 75497472 | bytes 75497472 | tf_op jit(solution)/shard_map/pallas_call | solution.py:97
  32.4 0.0 all-reduce.3.cloned.1.call-update
  32.5 0.0 copy-done
  32.5 0.0 copy-done.1
  32.5 28.1 %all_gather.6 = bf16[2048,16]{0,1:T(8,128)(2,1)S(1)} all-gather(bf16[256,16]{0,1:T(8,128)(2,1)S(1)} %multiply_convert_fusion), channel_id=1, replica_groups=mesh['owner'=4,'rows'=8] {'rows'}, dimensions={0}, use_global_device_ids=true | all-gather | bytes 73728 | tf_op jit(solution)/shard_map/all_gather | solution.py:137
  60.6 5.8 all_gather.7
  66.4 38.1 %all-reduce.3.cloned.1.call-done = (f32[16,1,1024]{2,1,0:T(1,128)}, f32[16,1,1024]{2,1,0:T(1,128)}, f32[16,1,1024]{2,1,0:T(1,128)}) async-done(((f32[16,1,1024]{2,1,0:T(1,128)}, f32[16,1,1024]{2,1,0:T(1,128)}, f32[16,1,1024]{2,1,0:T(1,128)}), (f32[16,1,1024]{2,1,0:T(1,128)}, f32[16,1,1024]{2,1,0:T(1,128)}, f32[16,1,1024]{2,1,0:T(1,128)})) %all-reduce.3.cloned.1.call-update) | async-done | bytes 196624 | tf_op jit(solution)/shard_map/pmax | solution.py:105
  104.5 35.8 %shard_map.136 = (bf16[8,16,256,128]{3,2,1,0:T(8,128)(2,1)}, bf16[8,16,256,128]{3,2,1,0:T(8,128)(2,1)}, bf16[8,16,128,256]{3,2,1,0:T(8,128)(2,1)}) custom-call(f32[16,256,1024]{2,1,0:T(8,128)} %tg.3, bf16[16,256,1024]{2,1,0:T(8,128)(2,1)} %og.3, f32[16,256,1024]{2,1,0:T(8,128)} %tu.3, bf16[16,256,1024]{2,1,0:T(8,128)(2,1)} %ou.3, f32[16,1024,256]{2,1,0:T(8,128)} %td.3, ...), custom_call_target="tpu_custom_call" | custom-call | flops 75497472 | bytes 150994944 | tf_op jit(solution)/shard_map/pallas_call | solution.py:108
  140.3 1.3 constant_dynamic-slice_fusion
  141.6 1.3 constant_dynamic-slice_fusion.2
  142.9 541.9 %shard_map.137 = (bf16[16,2048,128]{2,1,0:T(8,128)(2,1)}, bf16[16,2048,128]{2,1,0:T(8,128)(2,1)}, bf16[16,128,2048]{2,1,0:T(8,128)(2,1)}) custom-call(bf16[8,16,256,128]{3,2,1,0:T(8,128)(2,1)} %get-tuple-element.19.ng, bf16[8,16,256,128]{3,2,1,0:T(8,128)(2,1)} %get-tuple-element.20.nu, bf16[8,16,128,256]{3,2,1,0:T(8,128)(2,1)} %get-tuple-element.21.nd), custom_call_target="tpu_custom_call" | custom-call | tf_op jit(solution)/shard_map/pallas_call | solution.py:119
  684.8 7.6 %copy.22 = bf16[16,2048,128]{2,1,0:T(8,128)(2,1)} copy(bf16[16,2048,128]{2,1,0:T(8,128)(2,1)} %get-tuple-element.37) | data formatting | bytes 16777216
  692.4 7.6 %copy.23 = bf16[16,2048,128]{2,1,0:T(8,128)(2,1)} copy(bf16[16,2048,128]{2,1,0:T(8,128)(2,1)} %get-tuple-element.38) | data formatting | bytes 16777216
  699.9 8.4 %copy.24 = bf16[16,128,2048]{2,1,0:T(8,128)(2,1)} copy(bf16[16,128,2048]{2,1,0:T(8,128)(2,1)} %get-tuple-element.39) | data formatting | bytes 16777216
  708.4 0.7 copy.25
  (1 shorter events, 0.0 us)
Async XLA Ops:
  7.2 25.3 %copy-start = (f32[256,16]{0,1:T(8,128)S(1)}, f32[256,16]{0,1:T(8,128)}, u32[]{:S(2)}) copy-start(f32[256,16]{0,1:T(8,128)} %param.14) | copy-start | bytes 49156
  7.2 25.3 %copy-start.1 = (f32[256]{0:T(256)S(1)}, f32[256]{0:T(256)}, u32[]{:S(2)}) copy-start(f32[256]{0:T(256)} %param.15) | copy-start | bytes 3076
  7.2 97.3 %all-reduce.3.cloned.1.call-start = ((), (), s32[]{:S(2)}) async-start(), calls=%async_computation | async-start | bytes 393216 | tf_op jit(solution)/shard_map/pmax | solution.py:105
Sparse Core Ops, SparseCore 0:
  32.6 71.8 all-reduce.2
